TPU v7x, 32 devices: a whole 2x2x4 slice. The times are simulated.
32 devices in a mesh: enc: 8 (over z, x), dec: 2 (over y), grp: 2 (over core).
Axes of the slice: x: 2, y: 2, z: 4, core: 2. Of those that a mesh axis runs over, the one named last changes fastest.
Arguments:
- images: bfloat16 [32, 4, 32, 1280], P(('enc', 'dec', 'grp')), may hold values from -6 to 6
- ln_gain: float32 [1280], replicated, may hold values from 0.1 to 1.9
- ln_bias: float32 [1280], replicated, may hold values from -3 to 3
- fc1_weight: bfloat16 [5120, 1280], P('enc'), may hold values from -0.15625 to 0.15625
- fc1_bias: float32 [5120], P('enc'), may hold values from -3 to 3
- fc2_weight: bfloat16 [5120, 1280], P('enc'), may hold values from -0.078125 to 0.078125
- fc2_bias: float32 [1280], replicated, may hold values from -3 to 3
- key_weight: bfloat16 [1280, 512], replicated, may hold values from -0.15625 to 0.15625
- value_weight: bfloat16 [1280, 512], replicated, may hold values from -0.15625 to 0.15625
- text: bfloat16 [32, 128, 8192], P(('enc', 'grp')), may hold values from -6 to 6
- query_weight: bfloat16 [8192, 4096], P('enc', 'dec'), may hold values from -0.0625 to 0.0625
- tiles: int32 [8, 2, 2], replicated, may hold values from 1 to 4, as said below
- links: int32 [32, 2], P(('enc', 'grp')), may hold values from 0 to 1, as said below
- lengths: int32 [32], P(('enc', 'grp')), may hold values from 1 to 128
- state_grads: bfloat16 [32, 4, 32, 1280], P(('enc', 'dec', 'grp')), may hold values from -0.125 to 0.125
Outputs:
- context: bfloat16 [32, 128, 4096], P(('enc', 'grp'), None, 'dec')
- fc1_grad: float32 [5120, 1280], P(('enc', 'dec', 'grp'))
- fc2_grad: float32 [5120, 1280], P(('enc', 'dec', 'grp'))
Inputs may be any that keep to these rules, and one draw needn't show every extreme that they name: The 8 images that share their last two indices have 20 tiles together, and one of them has 4. `links`: every text is linked to at least one image.
All inputs are finite; a program needn't handle non-finite values.
Results may differ from a plain program's by a relative error of at most 0.017.
Values may be sent and summed in bfloat16 or wider, within the bound.
A program may use at most 128 MiB of HBM per device.

v0:
```python
import jax
import jax.numpy as jnp
from jax import lax
from jax.sharding import PartitionSpec as P

HEADS = 32
KV_HEADS = 4
HD = 128
EPSILON = 1e-06


def normalize_layer(values, gain, shift):
    middle = jnp.mean(values, axis=-1, keepdims=True)
    centered = values - middle
    spread = jnp.mean(centered * centered, axis=-1, keepdims=True)
    return centered * lax.rsqrt(spread + EPSILON) * gain + shift


def normalize_heads(values):
    return values * lax.rsqrt(jnp.mean(values * values, axis=-1, keepdims=True) + EPSILON)


def gelu_slope(values):
    return (
        0.5 * (1.0 + lax.erf(values * 0.7071067811865476))
        + values * jnp.exp(-0.5 * values * values) * 0.3989422804014327
    )


def encoder_rows(rows, fc1_weight, fc1_bias, fc2_weight):
    pre = (
        lax.dot_general(
            rows, fc1_weight, (((1,), (1,)), ((), ())), preferred_element_type=jnp.float32
        )
        + fc1_bias
    )
    hidden = jax.nn.gelu(pre, approximate=False).astype(jnp.bfloat16)
    partial_sum = jnp.dot(hidden, fc2_weight, preferred_element_type=jnp.float32)
    return (pre, hidden, partial_sum)


def weight_terms(rows, pre, hidden, cotangent, fc2_weight):
    hidden_grad = lax.dot_general(
        cotangent, fc2_weight, (((1,), (1,)), ((), ())), preferred_element_type=jnp.float32
    )
    second_term = lax.dot_general(
        hidden, cotangent, (((0,), (0,)), ((), ())), preferred_element_type=jnp.float32
    )
    pre_grad = (hidden_grad * gelu_slope(pre)).astype(jnp.bfloat16)
    first_term = lax.dot_general(
        pre_grad, rows, (((0,), (0,)), ((), ())), preferred_element_type=jnp.float32
    )
    return (first_term, second_term)


def project_heads(states, key_columns, value_columns, heads):
    width = states.shape[-1]
    key_raw = jnp.einsum(
        "rd,dhe->hre",
        states,
        key_columns.reshape(width, heads, HD),
        preferred_element_type=jnp.float32,
    )
    keys = normalize_heads(key_raw).astype(jnp.bfloat16)
    values = jnp.einsum(
        "rd,dhe->hre",
        states,
        value_columns.reshape(width, heads, HD),
        preferred_element_type=jnp.float32,
    ).astype(jnp.bfloat16)
    return (keys, values)


def on_device(
    images,
    ln_gain,
    ln_bias,
    fc1_weight,
    fc1_bias,
    fc2_weight,
    fc2_bias,
    key_weight,
    value_weight,
    text,
    query_weight,
    tiles,
    links,
    lengths,
    state_grads,
):
    dec_count = lax.axis_size("dec")
    grp_count = lax.axis_size("grp")
    enc_place = lax.axis_index("enc")
    dec_place = lax.axis_index("dec")
    grp_place = lax.axis_index("grp")
    slots = images.shape[1]
    patch = images.shape[2]
    width = images.shape[3]
    img_rows = slots * patch
    own_rows = images.reshape(img_rows, width)
    normed = normalize_layer(own_rows.astype(jnp.float32), ln_gain, ln_bias).astype(jnp.bfloat16)
    samples = text.shape[0]
    length = text.shape[1]
    text_rows = text.reshape(samples * length, text.shape[2])
    half = query_weight.shape[1] // grp_count
    own_half = lax.dynamic_slice_in_dim(query_weight, grp_place * half, half, 1)
    gathered, half_rows = (
        lax.all_gather(normed, "enc", axis=0, tiled=True),
        lax.all_gather(own_half, "enc", axis=0, tiled=True),
    )
    query_raw = jnp.dot(
        text_rows,
        lax.all_gather(half_rows, "grp", axis=1, tiled=True),
        preferred_element_type=jnp.float32,
    )
    tile_index = jnp.arange(slots)
    pre, hidden, partial_full = encoder_rows(gathered, fc1_weight, fc1_bias, fc2_weight)
    summed = lax.psum_scatter(
        partial_full.astype(jnp.bfloat16), "enc", scatter_dimension=0, tiled=True
    ).astype(jnp.float32)
    states = (own_rows.astype(jnp.float32) + summed + fc2_bias).astype(jnp.bfloat16)
    local_heads = query_weight.shape[1] // HD
    per_group = HEADS // KV_HEADS
    kv_local = max(1, local_heads // per_group)
    first_head = dec_place * local_heads // per_group
    key_columns = lax.dynamic_slice_in_dim(key_weight, first_head * HD, kv_local * HD, 1)
    value_columns = lax.dynamic_slice_in_dim(value_weight, first_head * HD, kv_local * HD, 1)
    piece = lax.all_gather(states.reshape(1, img_rows, width), "dec", axis=0, tiled=True)
    count = piece.shape[0]
    key_part, value_part = project_heads(
        piece.reshape(count * img_rows, width), key_columns, value_columns, kv_local
    )
    key_part = key_part.reshape(kv_local, count, img_rows, HD).transpose(1, 0, 2, 3)
    value_part = value_part.reshape(kv_local, count, img_rows, HD).transpose(1, 0, 2, 3)
    paired = jnp.stack([key_part, value_part])
    keys = paired[0]
    values = paired[1]
    heads_each = local_heads // kv_local
    queries = normalize_heads(query_raw.reshape(samples, length, local_heads, HD)).astype(
        jnp.bfloat16
    )
    queries = queries.reshape(samples, length, kv_local, heads_each, HD)
    dec_tiles = tiles[enc_place, :, grp_place]
    live_keys = tile_index[None, :] < dec_tiles[:, None]
    live_keys = jnp.broadcast_to(live_keys[:, :, None], (dec_count, slots, patch)).reshape(
        dec_count, img_rows
    )
    allowed = (links[:, :, None] > 0) & live_keys[None, :, :]
    scores = jnp.einsum(
        "sqghd,jgkd->sghjkq", queries, keys, preferred_element_type=jnp.float32
    ) * HD ** (-0.5)
    weights = jnp.where(allowed[:, None, None, :, :, None], jnp.exp(scores), 0.0)
    totals = jnp.sum(weights, axis=(3, 4), keepdims=True)
    probs = (weights / totals).astype(jnp.bfloat16)
    mixed = jnp.einsum("sghjkq,jgkd->sqghd", probs, values, preferred_element_type=jnp.float32)
    valid = jnp.arange(length)[None, :] < lengths[:, None]
    context = (
        jnp.where(valid[:, :, None, None, None], mixed, 0.0)
        .reshape(samples, length, local_heads * HD)
        .astype(jnp.bfloat16)
    )
    own_tiles = tiles[enc_place, dec_place, grp_place]
    own_live = jnp.broadcast_to((tile_index < own_tiles)[:, None, None], (slots, patch, 1)).reshape(
        img_rows, 1
    )
    cotangent = jnp.where(
        own_live, state_grads.reshape(img_rows, width), jnp.zeros((), state_grads.dtype)
    )
    all_cotangent = lax.all_gather(cotangent, "enc", axis=0, tiled=True)
    first_term, second_term = weight_terms(gathered, pre, hidden, all_cotangent, fc2_weight)
    fc1_grad, fc2_grad = (
        lax.psum_scatter(
            first_term.astype(jnp.bfloat16), ("dec", "grp"), scatter_dimension=0, tiled=True
        ).astype(jnp.float32),
        lax.psum_scatter(
            second_term.astype(jnp.bfloat16), ("dec", "grp"), scatter_dimension=0, tiled=True
        ).astype(jnp.float32),
    )
    return (context, fc1_grad, fc2_grad)


def solution(mesh):
    in_specs = (
        P(("enc", "dec", "grp"), None, None, None),
        P(),
        P(),
        P("enc", None),
        P("enc"),
        P("enc", None),
        P(),
        P(),
        P(),
        P(("enc", "grp"), None, None),
        P("enc", "dec"),
        P(),
        P(("enc", "grp"), None),
        P(("enc", "grp")),
        P(("enc", "dec", "grp"), None, None, None),
    )
    out_specs = (
        P(("enc", "grp"), None, "dec"),
        P(("enc", "dec", "grp"), None),
        P(("enc", "dec", "grp"), None),
    )
    return jax.shard_map(
        on_device, mesh=mesh, in_specs=in_specs, out_specs=out_specs, check_vma=False
    )
```

profile of v0, /device:TPU:0, one launch (start us, length us, event | category | flops | bytes accessed | tf_op | source)
XLA Modules:
  0.0 579.2 jit_solution(997100307381949104)
XLA Ops:
  7.2 1.2 convert_reduce_fusion
  8.4 0.1 div.40
  8.5 1.2 fusion.29
  9.8 0.1 rsqrt.31
  9.8 2.0 fusion.33
  11.9 1.3 dynamic_slice.19
  13.2 0.6 iota_compare_fusion.2
  13.8 0.1 broadcast_in_dim.70
  13.9 0.1 broadcast_in_dim.71
  14.0 1.8 bitcast_select_fusion.2
  15.9 3.3 constant_dynamic-slice_fusion
  19.2 49.9 %all-gather.6.cloned.1.call-done = bf16[1024,1280]{1,0:T(8,128)(2,1)} async-done(((bf16[128,1280]{1,0:T(8,128)(2,1)}), bf16[1024,1280]{1,0:T(8,128)(2,1)}) %all-gather.6.cloned.1.call-update) | async-done | bytes 2621456 | tf_op jit(solution)/shard_map/all_gather | solution.py:108
  69.1 10.1 %fusion.3 = (bf16[1024,640]{1,0:T(8,128)(2,1)}, f32[1024,640]{1,0:T(8,128)}) fusion(f32[640]{0:T(1024)S(1)} %copy-done.6, bf16[1024,1280]{1,0:T(8,128)(2,1)} %all-gather.6.cloned.1.call-done, bf16[640,1280]{1,0:T(8,128)(2,1)S(1)} %copy-done.5), kind=kOutput, calls=%fused_computation.11 | convolution fusion | flops 1720975360 | bytes 8194560 | tf_op jit(solution)/shard_map/dot_general | solution.py:32
  79.2 45.7 %all-gather.12.cloned.1.call-done = bf16[1024,1280]{1,0:T(8,128)(2,1)} async-done(((bf16[128,1280]{1,0:T(8,128)(2,1)}), bf16[1024,1280]{1,0:T(8,128)(2,1)}) %all-gather.12.cloned.1.call-update) | async-done | bytes 2621456 | tf_op jit(solution)/shard_map/all_gather | solution.py:169
  124.9 11.8 %convolution_convert_fusion.2 = bf16[640,1280]{1,0:T(8,128)(2,1)} fusion(bf16[1024,1280]{1,0:T(8,128)(2,1)} %all-gather.6.cloned.1.call-done, f32[1024,640]{1,0:T(8,128)} %get-tuple-element.13, bf16[1024,1280]{1,0:T(8,128)(2,1)} %all-gather.12.cloned.1.call-done, bf16[640,1280]{1,0:T(8,128)(2,1)S(1)} %copy-done, f32[640]{0:T(1024)S(1)} %copy-done.6), kind=kOutput, calls=%fused_computation.7 | convolution fusion | flops 3363471360 | bytes 11143680 | tf_op jit(solution)/shard_map/dot_general | solution.py:50
  136.7 5.2 convolution_convert_fusion.1
  142.0 0.2 reduce-scatter.4.cloned.1.call-start
  142.2 3.7 convolution_convert_fusion
  146.0 206.9 %all-gather.8.cloned.1.call-done = bf16[8192,1024]{1,0:T(8,128)(2,1)} async-done(((bf16[1024,1024]{1,0:T(8,128)(2,1)}), bf16[8192,1024]{1,0:T(8,128)(2,1)}) %all-gather.8.cloned.1.call-update) | async-done | bytes 16777232 | tf_op jit(solution)/shard_map/all_gather | solution.py:109
  353.0 0.6 copy-done.7
  353.6 0.1 copy.48
  353.7 0.2 dynamic-slice_reduce_fusion
  353.9 0.1 iota_compare_fusion
  354.0 0.1 broadcast_in_dim.39
  354.1 0.1 and.29
  354.1 1.4 constant_dynamic-slice_fusion.1
  355.6 0.2 copy.49
  355.8 0.2 copy.46
  356.1 0.1 broadcast_and_fusion
  356.2 25.8 %reduce-scatter.6.cloned.1.call-done = bf16[160,1280]{1,0:T(8,128)(2,1)} async-done(((bf16[640,1280]{1,0:T(8,128)(2,1)}), bf16[160,1280]{1,0:T(8,128)(2,1)}) %reduce-scatter.6.cloned.1.call-update) | async-done | bytes 409616 | tf_op jit(solution)/shard_map/reduce_scatter | solution.py:172
  382.0 1.9 convert_element_type.88
  384.0 28.9 %reduce-scatter.8.cloned.1.call-done = bf16[160,1280]{1,0:T(8,128)(2,1)} async-done(((bf16[640,1280]{1,0:T(8,128)(2,1)}), bf16[160,1280]{1,0:T(8,128)(2,1)}) %reduce-scatter.8.cloned.1.call-update) | async-done | bytes 409616 | tf_op jit(solution)/shard_map/reduce_scatter | solution.py:175
  412.8 1.9 convert_element_type.90
  414.8 72.4 %reduce-scatter.4.cloned.1.call-done = bf16[128,1280]{1,0:T(8,128)(2,1)} async-done(((bf16[1024,1280]{1,0:T(8,128)(2,1)}), bf16[128,1280]{1,0:T(8,128)(2,1)}) %reduce-scatter.4.cloned.1.call-update) | async-done | bytes 327696 | tf_op jit(solution)/shard_map/reduce_scatter | solution.py:118
  487.2 1.1 fusion.35
  488.3 8.7 %all-gather = bf16[256,1280]{1,0:T(8,128)(2,1)S(1)} all-gather(bf16[128,1280]{1,0:T(8,128)(2,1)S(1)} %fusion.35), channel_id=2, replica_groups=mesh['enc'=8,'dec'=2,'grp'=2] {'dec'}, dimensions={0}, use_global_device_ids=true | all-gather | bytes 983040 | tf_op jit(solution)/shard_map/all_gather | solution.py:128
  497.0 0.4 multiply_reduce_fusion
  497.4 0.1 copy.61
  497.5 0.4 fusion.20
  497.9 41.0 %all-gather.10.cloned.1.call-done = bf16[8192,2048]{1,0:T(8,128)(2,1)} async-done(((bf16[8192,1024]{1,0:T(8,128)(2,1)}), bf16[8192,2048]{1,0:T(8,128)(2,1)}) %all-gather.10.cloned.1.call-update) | async-done | bytes 33554448 | tf_op jit(solution)/shard_map/all_gather | solution.py:113
  538.9 17.7 %fusion.48 = (f32[256,2048]{0,1:T(8,128)}, f32[256,2048]{0,1:T(8,128)}) fusion(bf16[8192,2048]{1,0:T(8,128)(2,1)} %all-gather.10.cloned.1.call-done, bf16[256,8192]{1,0:T(8,128)(2,1)} %bitcast.111), kind=kOutput, calls=%fused_computation.87 | convolution fusion | flops 8590458880 | bytes 41943040 | tf_op jit(solution)/shard_map/dot_general | solution.py:111
  556.6 2.3 mul.116
  558.9 3.3 reshape.170
  562.2 4.1 copy.53
  566.3 0.6 reduce_sum.48
  566.9 2.9 fusion
  569.8 1.2 fusion.19
  571.1 1.3 copy.56
  (39 shorter events, 0.6 us)
Async XLA Ops:
  7.2 117.7 %copy-start = (bf16[640,1280]{1,0:T(8,128)(2,1)S(1)}, bf16[640,1280]{1,0:T(8,128)(2,1)}, u32[]{:S(2)}) copy-start(bf16[640,1280]{1,0:T(8,128)(2,1)} %param.20) | copy-start | bytes 4915204
  7.2 61.9 %all-gather.6.cloned.1.call-start = ((), (), s32[]{:S(2)}) async-start(), calls=%async_computation.3 | async-start | bytes 2949120 | tf_op jit(solution)/shard_map/all_gather | solution.py:108
  11.8 113.0 %all-gather.12.cloned.1.call-start = ((), (), s32[]{:S(2)}) async-start(), calls=%async_computation.7 | async-start | bytes 2949120 | tf_op jit(solution)/shard_map/all_gather | solution.py:169
  15.8 337.1 %all-gather.8.cloned.1.call-start = ((), (), s32[]{:S(2)}) async-start(), calls=%async_computation.5 | async-start | bytes 18874368 | tf_op jit(solution)/shard_map/all_gather | solution.py:109
  15.9 53.3 %copy-start.5 = (bf16[640,1280]{1,0:T(8,128)(2,1)S(1)}, bf16[640,1280]{1,0:T(8,128)(2,1)}, u32[]{:S(2)}) copy-start(bf16[640,1280]{1,0:T(8,128)(2,1)} %param.18) | copy-start | bytes 4915204
  15.9 53.3 %copy-start.6 = (f32[640]{0:T(1024)S(1)}, f32[640]{0:T(1024)}, u32[]{:S(2)}) copy-start(f32[640]{0:T(1024)} %param.19) | copy-start | bytes 7684
  19.2 362.8 %reduce-scatter.6.cloned.1.call-start = ((), (), s32[]{:S(2)}) async-start(), calls=%async_computation.8 | async-start | bytes 2048000 | tf_op jit(solution)/shard_map/reduce_scatter | solution.py:172
  124.9 11.8 %copy-start.9 = (bf16[1024,640]{1,0:T(8,128)(2,1)S(1)}, bf16[1024,640]{1,0:T(8,128)(2,1)}, u32[]{:S(2)}) copy-start(bf16[1024,640]{1,0:T(8,128)(2,1)} %get-tuple-element.12) | copy-start | bytes 3932164
  136.7 276.2 %reduce-scatter.8.cloned.1.call-start = ((), (), s32[]{:S(2)}) async-start(), calls=%async_computation.9 | async-start | bytes 2048000 | tf_op jit(solution)/shard_map/reduce_scatter | solution.py:175
  142.0 345.2 %reduce-scatter.4.cloned.1.call-start = ((), (), s32[]{:S(2)}) async-start(), calls=%async_computation.4 | async-start | bytes 2949120 | tf_op jit(solution)/shard_map/reduce_scatter | solution.py:118
  145.9 393.0 %all-gather.10.cloned.1.call-start = ((), (), s32[]{:S(2)}) async-start(), calls=%async_computation.6 | async-start | bytes 50331648 | tf_op jit(solution)/shard_map/all_gather | solution.py:113
  352.9 0.7 copy-start.7
  352.9 0.8 copy-start.4
  354.1 1.9 copy-start.8
  355.5 131.6 %copy-start.2 = (bf16[1,4,32,1280]{3,2,1,0:T(8,128)(2,1)S(1)}, bf16[1,4,32,1280]{3,2,1,0:T(8,128)(2,1)}, u32[]{:S(2)}) copy-start(bf16[1,4,32,1280]{3,2,1,0:T(8,128)(2,1)} %param.15) | copy-start | bytes 983044
  355.6 131.6 %copy-start.3 = (f32[1280]{0:T(1024)S(1)}, f32[1280]{0:T(1024)}, u32[]{:S(2)}) copy-start(f32[1280]{0:T(1024)} %param.21) | copy-start | bytes 15364
  569.8 2.6 copy-start.1
Sparse Core Ops, SparseCore 0:
  12.0 57.1 all-gather.5
  71.9 52.9 all-gather.11
  127.0 225.8 all-gather.7
  355.3 26.6 reduce-scatter.5
  384.4 28.3 reduce-scatter.7
  416.2 70.9 reduce-scatter.3
  488.7 50.1 all-gather.9
where the time goes:
time: 580 us; the launch traced here: 579 us
  waiting for transfers between devices  471 us (81%)
  matrix products  53.3 us (9%)
  local copies, waits for them, and re-layouts  19.1 us (3%)
  between operations  14.3 us (2%)
  other arithmetic  12.6 us (2%)
  blocking collectives  8.7 us (1%)
    all_gather x1, waiting for transfers between devices, on_device(): lax.all_gather(own_half, 'enc', axis=0, tiled=True)  207 us
    reduce_scatter x1, waiting for transfers between devices, on_device(): lax.psum_scatter(partial_full.astype(jnp.bfloat16), 'enc', scatter_dimens...  72.4 us
    all_gather x1, waiting for transfers between devices, on_device(): lax.all_gather(normed, 'enc', axis=0, tiled=True)  49.9 us
    all_gather x1, waiting for transfers between devices, on_device(): all_cotangent = lax.all_gather(cotangent, 'enc', axis=0, tiled=True)  45.7 us
    all_gather x1, waiting for transfers between devices, on_device(): lax.all_gather(half_rows, 'grp', axis=1, tiled=True)  41 us
    reduce_scatter x1, waiting for transfers between devices, on_device(): lax.psum_scatter(second_term.astype(jnp.bfloat16), ('dec', 'grp'), scatte...  28.9 us
    reduce_scatter x1, waiting for transfers between devices, on_device(): lax.psum_scatter(first_term.astype(jnp.bfloat16), ('dec', 'grp'), scatter...  25.8 us
    dot_general x1, matrix products, on_device(): jnp.dot(text_rows, lax.all_gather(half_rows, 'grp', axis=1, tiled=True),...  17.7 us
  transfers between devices with their start and end apart: 7, of which 7 were waited for; matrix products, arithmetic and copies ran while one was open for 8% of the time, Pallas kernels for 0%

commit v1 on v0

--- a/solution.py
+++ b/solution.py
@@ -166,7 +166,12 @@
     cotangent = jnp.where(
         own_live, state_grads.reshape(img_rows, width), jnp.zeros((), state_grads.dtype)
     )
-    all_cotangent = lax.all_gather(cotangent, "enc", axis=0, tiled=True)
+    ring = [cotangent]
+    for hop in range(7):
+        ring.append(lax.ppermute(ring[-1], "enc", [(dev, (dev + 1) % 8) for dev in range(8)]))
+    all_cotangent = jnp.roll(
+        jnp.concatenate(ring[::-1], axis=0), (lax.axis_index("enc") + 1) * ring[0].shape[0], axis=0
+    )
     first_term, second_term = weight_terms(gathered, pre, hidden, all_cotangent, fc2_weight)
     fc1_grad, fc2_grad = (
         lax.psum_scatter(

time: 580 us -> 551 us (0.950)
  waiting for transfers between devices: 471 us -> 425 us
  local copies, waits for them, and re-layouts: 19.1 us -> 35 us
    ppermute x0 -> x7, waiting for transfers between devices: none -> 111 us  [on_device(): lax.ppermute(ring[-1], 'enc', [(dev, (dev + 1) % 8) for dev in range(8)])]
    all_gather x1, waiting for transfers between devices: 207 us -> 146 us  [on_device(): lax.all_gather(own_half, 'enc', axis=0, tiled=True)]
    all_gather x1, waiting for transfers between devices: 49.9 us -> 0.01 us  [on_device(): lax.all_gather(normed, 'enc', axis=0, tiled=True)]
    all_gather x1 -> x0, waiting for transfers between devices: 45.7 us -> none  [on_device(): all_cotangent = lax.all_gather(cotangent, 'enc', axis=0, tiled=True)]
    unnamed x21 -> x36, local copies, waits for them, and re-layouts: 2 us -> 19.7 us
  transfers between devices with their start and end apart: 7 -> 13, of which waited for: 7 -> 12; matrix products, arithmetic and copies ran while one was open for 8% -> 11% of each run, Pallas kernels for 0% -> 0%
where the time goes in v1:
time: 551 us; the launch traced here: 550 us
  waiting for transfers between devices  425 us (77%)
  matrix products  51.3 us (9%)
  local copies, waits for them, and re-layouts  35 us (6%)
  between operations  14.3 us (3%)
  other arithmetic  12.5 us (2%)
  blocking collectives  8.7 us (2%)
    all_gather x1, waiting for transfers between devices, on_device(): lax.all_gather(own_half, 'enc', axis=0, tiled=True)  146 us
    ppermute x7, waiting for transfers between devices, on_device(): lax.ppermute(ring[-1], 'enc', [(dev, (dev + 1) % 8) for dev in range(8)])  111 us
    reduce_scatter x1, waiting for transfers between devices, on_device(): lax.psum_scatter(partial_full.astype(jnp.bfloat16), 'enc', scatter_dimens...  72.5 us
    all_gather x1, waiting for transfers between devices, on_device(): lax.all_gather(half_rows, 'grp', axis=1, tiled=True)  40.9 us
    reduce_scatter x1, waiting for transfers between devices, on_device(): lax.psum_scatter(second_term.astype(jnp.bfloat16), ('dec', 'grp'), scatte...  28.9 us
    reduce_scatter x1, waiting for transfers between devices, on_device(): lax.psum_scatter(first_term.astype(jnp.bfloat16), ('dec', 'grp'), scatter...  25.5 us
    unnamed x36, local copies, waits for them, and re-layouts  19.7 us
    dot_general x1, matrix products, on_device(): jnp.dot(text_rows, lax.all_gather(half_rows, 'grp', axis=1, tiled=True),...  17.3 us
  transfers between devices with their start and end apart: 13, of which 12 were waited for; matrix products, arithmetic and copies ran while one was open for 11% of the time, Pallas kernels for 0%

profile of v1, /device:TPU:0, one launch (start us, length us, event | category | flops | bytes accessed | tf_op | source)
XLA Modules:
  0.0 550.2 jit_solution(2436843301166025568)
XLA Ops:
  7.2 1.2 convert_reduce_fusion
  8.4 1.2 fusion.36
  9.8 2.0 fusion.40
  11.9 3.1 constant_dynamic-slice_fusion
  16.7 3.0 collective-permute-start
  19.7 13.7 %collective-permute-done = bf16[128,1280]{1,0:T(8,128)(2,1)S(1)} collective-permute-done((bf16[128,1280]{1,0:T(8,128)(2,1)S(1)}, bf16[128,1280]{1,0:T(8,128)(2,1)S(1)}, u32[]{:S(2)}, u32[]{:S(2)}) %collective-permute-start) | collective-permute-done | bytes 327712 | tf_op jit(solution)/shard_map/ppermute | solution.py:171
  33.4 14.6 %collective-permute-done.1 = bf16[128,1280]{1,0:T(8,128)(2,1)S(1)} collective-permute-done((bf16[128,1280]{1,0:T(8,128)(2,1)S(1)}, bf16[128,1280]{1,0:T(8,128)(2,1)S(1)}, u32[]{:S(2)}, u32[]{:S(2)}) %collective-permute-start.1) | collective-permute-done | bytes 327712 | tf_op jit(solution)/shard_map/ppermute | solution.py:171
  48.1 19.1 %collective-permute-done.2 = bf16[128,1280]{1,0:T(8,128)(2,1)S(1)} collective-permute-done((bf16[128,1280]{1,0:T(8,128)(2,1)S(1)}, bf16[128,1280]{1,0:T(8,128)(2,1)S(1)}, u32[]{:S(2)}, u32[]{:S(2)}) %collective-permute-start.2) | collective-permute-done | bytes 327712 | tf_op jit(solution)/shard_map/ppermute | solution.py:171
  67.2 19.0 %collective-permute-done.3 = bf16[128,1280]{1,0:T(8,128)(2,1)S(1)} collective-permute-done((bf16[128,1280]{1,0:T(8,128)(2,1)S(1)}, bf16[128,1280]{1,0:T(8,128)(2,1)S(1)}, u32[]{:S(2)}, u32[]{:S(2)}) %collective-permute-start.3) | collective-permute-done | bytes 327712 | tf_op jit(solution)/shard_map/ppermute | solution.py:171
  86.2 9.9 %collective-permute-done.4 = bf16[128,1280]{1,0:T(8,128)(2,1)} collective-permute-done((bf16[128,1280]{1,0:T(8,128)(2,1)S(1)}, bf16[128,1280]{1,0:T(8,128)(2,1)}, u32[]{:S(2)}, u32[]{:S(2)}) %collective-permute-start.4) | collective-permute-done | bytes 327712 | tf_op jit(solution)/shard_map/ppermute | solution.py:171
  96.1 17.0 %collective-permute-done.5 = bf16[128,1280]{1,0:T(8,128)(2,1)} collective-permute-done((bf16[128,1280]{1,0:T(8,128)(2,1)}, bf16[128,1280]{1,0:T(8,128)(2,1)}, u32[]{:S(2)}, u32[]{:S(2)}) %collective-permute-start.5) | collective-permute-done | bytes 327712 | tf_op jit(solution)/shard_map/ppermute | solution.py:171
  113.1 17.2 %collective-permute-done.6 = bf16[128,1280]{1,0:T(8,128)(2,1)} collective-permute-done((bf16[128,1280]{1,0:T(8,128)(2,1)}, bf16[128,1280]{1,0:T(8,128)(2,1)}, u32[]{:S(2)}, u32[]{:S(2)}) %collective-permute-start.6) | collective-permute-done | bytes 327712 | tf_op jit(solution)/shard_map/ppermute | solution.py:171
  130.3 1.7 constant_dynamic-update-slice_fusion.15
  132.0 1.7 constant_dynamic-update-slice_fusion.14
  133.7 1.7 constant_dynamic-update-slice_fusion.13
  135.4 0.8 constant_dynamic-update-slice_fusion.12
  136.2 0.7 constant_dynamic-update-slice_fusion.11
  136.9 0.7 constant_dynamic-update-slice_fusion.10
  139.2 1.8 constant_dynamic-update-slice_fusion.7
  140.9 1.7 constant_dynamic-update-slice_fusion.6
  142.6 1.7 constant_dynamic-update-slice_fusion.5
  144.4 0.8 constant_dynamic-update-slice_fusion.4
  145.9 0.8 constant_dynamic-update-slice_fusion.2
  146.6 0.8 constant_dynamic-update-slice_fusion.1
  147.4 0.7 constant_dynamic-update-slice_fusion
  148.1 10.4 %fusion.3 = (bf16[1024,640]{1,0:T(8,128)(2,1)S(1)}, f32[1024,640]{1,0:T(8,128)}) fusion(f32[640]{0:T(1024)S(1)} %copy-done.7, bf16[1024,1280]{1,0:T(8,128)(2,1)} %all-gather.5.cloned.1.call-done, bf16[640,1280]{1,0:T(8,128)(2,1)} %param.18), kind=kOutput, calls=%fused_computation.11 | convolution fusion | flops 1720975360 | bytes 8194560 | tf_op jit(solution)/shard_map/dot_general | solution.py:32
  158.5 11.7 %convolution_convert_fusion.2 = bf16[640,1280]{1,0:T(8,128)(2,1)} fusion(bf16[1024,1280]{1,0:T(8,128)(2,1)} %all-gather.5.cloned.1.call-done, f32[1024,640]{1,0:T(8,128)} %get-tuple-element.13, bf16[640,1280]{1,0:T(8,128)(2,1)S(1)} %copy-done, bf16[2048,1280]{1,0:T(8,128)(2,1)} %constant_dynamic-update-slice_fusion, s32[]{:T(128)S(6)} %select_n.58, ...), kind=kOutput, calls=%fused_computation.7 | convolution fusion | flops 3363471360 | bytes 11143684 | tf_op jit(solution)/shard_map/dot_general | solution.py:50
  170.4 4.8 convolution_convert_fusion.1
  175.3 3.7 convolution_convert_fusion
  179.1 146.5 %all-gather.7.cloned.1.call-done = bf16[8192,1024]{1,0:T(8,128)(2,1)} async-done(((bf16[1024,1024]{1,0:T(8,128)(2,1)}), bf16[8192,1024]{1,0:T(8,128)(2,1)}) %all-gather.7.cloned.1.call-update) | async-done | bytes 16777232 | tf_op jit(solution)/shard_map/all_gather | solution.py:109
  325.6 1.3 copy-done.4
  326.9 1.2 constant_dynamic-slice_fusion.1
  329.3 25.5 %reduce-scatter.6.cloned.1.call-done = bf16[160,1280]{1,0:T(8,128)(2,1)} async-done(((bf16[640,1280]{1,0:T(8,128)(2,1)}), bf16[160,1280]{1,0:T(8,128)(2,1)}) %reduce-scatter.6.cloned.1.call-update) | async-done | bytes 409616 | tf_op jit(solution)/shard_map/reduce_scatter | solution.py:177
  354.8 1.9 convert_element_type.88
  356.7 28.9 %reduce-scatter.8.cloned.1.call-done = bf16[160,1280]{1,0:T(8,128)(2,1)} async-done(((bf16[640,1280]{1,0:T(8,128)(2,1)}), bf16[160,1280]{1,0:T(8,128)(2,1)}) %reduce-scatter.8.cloned.1.call-update) | async-done | bytes 409616 | tf_op jit(solution)/shard_map/reduce_scatter | solution.py:180
  385.6 1.9 convert_element_type.90
  387.6 72.5 %reduce-scatter.4.cloned.1.call-done = bf16[128,1280]{1,0:T(8,128)(2,1)} async-done(((bf16[1024,1280]{1,0:T(8,128)(2,1)}), bf16[128,1280]{1,0:T(8,128)(2,1)}) %reduce-scatter.4.cloned.1.call-update) | async-done | bytes 327696 | tf_op jit(solution)/shard_map/reduce_scatter | solution.py:118
  460.1 1.1 fusion.42
  461.2 8.7 %all-gather = bf16[256,1280]{1,0:T(8,128)(2,1)S(1)} all-gather(bf16[128,1280]{1,0:T(8,128)(2,1)S(1)} %fusion.42), channel_id=2, replica_groups=mesh['enc'=8,'dec'=2,'grp'=2] {'dec'}, dimensions={0}, use_global_device_ids=true | all-gather | bytes 983040 | tf_op jit(solution)/shard_map/all_gather | solution.py:128
  470.8 40.9 %all-gather.9.cloned.1.call-done = bf16[8192,2048]{1,0:T(8,128)(2,1)} async-done(((bf16[8192,1024]{1,0:T(8,128)(2,1)}), bf16[8192,2048]{1,0:T(8,128)(2,1)}) %all-gather.9.cloned.1.call-update) | async-done | bytes 33554448 | tf_op jit(solution)/shard_map/all_gather | solution.py:113
  511.6 17.3 %fusion.59 = (f32[256,2048]{0,1:T(8,128)}, f32[256,2048]{0,1:T(8,128)S(1)}) fusion(bf16[8192,2048]{1,0:T(8,128)(2,1)} %all-gather.9.cloned.1.call-done, bf16[256,8192]{1,0:T(8,128)(2,1)} %bitcast.109), kind=kOutput, calls=%fused_computation.109 | convolution fusion | flops 8590458880 | bytes 41943040 | tf_op jit(solution)/shard_map/dot_general | solution.py:111
  528.9 2.1 reshape.170
  531.0 2.8 copy.53
  533.8 3.3 mul.119
  537.1 2.1 reduce_sum.48
  539.2 1.5 fusion
  540.8 1.2 fusion.24
  542.1 1.3 copy.56
  (66 shorter events, 6.6 us)
Async XLA Ops:
  7.2 151.3 %copy-start = (bf16[640,1280]{1,0:T(8,128)(2,1)S(1)}, bf16[640,1280]{1,0:T(8,128)(2,1)}, u32[]{:S(2)}) copy-start(bf16[640,1280]{1,0:T(8,128)(2,1)} %param.20) | copy-start | bytes 4915204
  7.2 140.9 %all-gather.5.cloned.1.call-start = ((), (), s32[]{:S(2)}) async-start(), calls=%async_computation.3 | async-start | bytes 2949120 | tf_op jit(solution)/shard_map/all_gather | solution.py:108
  11.8 313.7 %all-gather.7.cloned.1.call-start = ((), (), s32[]{:S(2)}) async-start(), calls=%async_computation.5 | async-start | bytes 18874368 | tf_op jit(solution)/shard_map/all_gather | solution.py:109
  11.9 3.3 copy-start.6
  11.9 4.7 copy-start.3
  15.1 339.7 %reduce-scatter.6.cloned.1.call-start = ((), (), s32[]{:S(2)}) async-start(), calls=%async_computation.7 | async-start | bytes 2048000 | tf_op jit(solution)/shard_map/reduce_scatter | solution.py:177
  16.7 16.7 %collective-permute-start = (bf16[128,1280]{1,0:T(8,128)(2,1)S(1)}, bf16[128,1280]{1,0:T(8,128)(2,1)S(1)}, u32[]{:S(2)}, u32[]{:S(2)}) collective-permute-start(bf16[128,1280]{1,0:T(8,128)(2,1)S(1)} %bitcast_select_fusion.2), channel_id=1, source_target_pairs={{0,4},{4,8},{8,12},{12,16},{16,20},{20,24},{24,28},{28,0},{1,5},{5... | collective-permute-start | bytes 983048 | tf_op jit(solution)/shard_map/ppermute | solution.py:171
  33.4 14.6 %collective-permute-start.1 = (bf16[128,1280]{1,0:T(8,128)(2,1)S(1)}, bf16[128,1280]{1,0:T(8,128)(2,1)S(1)}, u32[]{:S(2)}, u32[]{:S(2)}) collective-permute-start(bf16[128,1280]{1,0:T(8,128)(2,1)S(1)} %collective-permute-done), channel_id=1, source_target_pairs={{0,4},{4,8},{8,12},{12,16},{16,20},{20,24},{24,28},{28,0},{1,5},{5... | collective-permute-start | bytes 983048 | tf_op jit(solution)/shard_map/ppermute | solution.py:171
  48.0 19.1 %collective-permute-start.2 = (bf16[128,1280]{1,0:T(8,128)(2,1)S(1)}, bf16[128,1280]{1,0:T(8,128)(2,1)S(1)}, u32[]{:S(2)}, u32[]{:S(2)}) collective-permute-start(bf16[128,1280]{1,0:T(8,128)(2,1)S(1)} %collective-permute-done.1), channel_id=1, source_target_pairs={{0,4},{4,8},{8,12},{12,16},{16,20},{20,24},{24,28},{28,0},{1,5},{5... | collective-permute-start | bytes 983048 | tf_op jit(solution)/shard_map/ppermute | solution.py:171
  67.2 19.0 %collective-permute-start.3 = (bf16[128,1280]{1,0:T(8,128)(2,1)S(1)}, bf16[128,1280]{1,0:T(8,128)(2,1)S(1)}, u32[]{:S(2)}, u32[]{:S(2)}) collective-permute-start(bf16[128,1280]{1,0:T(8,128)(2,1)S(1)} %collective-permute-done.2), channel_id=1, source_target_pairs={{0,4},{4,8},{8,12},{12,16},{16,20},{20,24},{24,28},{28,0},{1,5},{5... | collective-permute-start | bytes 983048 | tf_op jit(solution)/shard_map/ppermute | solution.py:171
  86.2 9.9 %collective-permute-start.4 = (bf16[128,1280]{1,0:T(8,128)(2,1)S(1)}, bf16[128,1280]{1,0:T(8,128)(2,1)}, u32[]{:S(2)}, u32[]{:S(2)}) collective-permute-start(bf16[128,1280]{1,0:T(8,128)(2,1)S(1)} %collective-permute-done.3), channel_id=1, source_target_pairs={{0,4},{4,8},{8,12},{12,16},{16,20},{20,24},{24,28},{28,0},{1,5},{5... | collective-permute-start | bytes 983048 | tf_op jit(solution)/shard_map/ppermute | solution.py:171
  96.1 17.0 %collective-permute-start.5 = (bf16[128,1280]{1,0:T(8,128)(2,1)}, bf16[128,1280]{1,0:T(8,128)(2,1)}, u32[]{:S(2)}, u32[]{:S(2)}) collective-permute-start(bf16[128,1280]{1,0:T(8,128)(2,1)} %collective-permute-done.4), channel_id=1, source_target_pairs={{0,4},{4,8},{8,12},{12,16},{16,20},{20,24},{24,28},{28,0},{1,5},{5... | collective-permute-start | bytes 983048 | tf_op jit(solution)/shard_map/ppermute | solution.py:171
  113.1 17.2 %collective-permute-start.6 = (bf16[128,1280]{1,0:T(8,128)(2,1)}, bf16[128,1280]{1,0:T(8,128)(2,1)}, u32[]{:S(2)}, u32[]{:S(2)}) collective-permute-start(bf16[128,1280]{1,0:T(8,128)(2,1)} %collective-permute-done.5), channel_id=1, source_target_pairs={{0,4},{4,8},{8,12},{12,16},{16,20},{20,24},{24,28},{28,0},{1,5},{5... | collective-permute-start | bytes 983048 | tf_op jit(solution)/shard_map/ppermute | solution.py:171
  139.2 9.0 %copy-start.7 = (f32[640]{0:T(1024)S(1)}, f32[640]{0:T(1024)}, u32[]{:S(2)}) copy-start(f32[640]{0:T(1024)} %param.19) | copy-start | bytes 7684
  170.2 215.4 %reduce-scatter.8.cloned.1.call-start = ((), (), s32[]{:S(2)}) async-start(), calls=%async_computation.8 | async-start | bytes 2048000 | tf_op jit(solution)/shard_map/reduce_scatter | solution.py:180
  175.3 284.8 %reduce-scatter.4.cloned.1.call-start = ((), (), s32[]{:S(2)}) async-start(), calls=%async_computation.4 | async-start | bytes 2949120 | tf_op jit(solution)/shard_map/reduce_scatter | solution.py:118
  179.0 332.6 %all-gather.9.cloned.1.call-start = ((), (), s32[]{:S(2)}) async-start(), calls=%async_computation.6 | async-start | bytes 50331648 | tf_op jit(solution)/shard_map/all_gather | solution.py:113
  325.5 1.3 copy-start.4
  325.6 3.2 copy-start.8
  326.9 2.3 copy-start.9
  328.1 132.0 %copy-start.2 = (bf16[1,4,32,1280]{3,2,1,0:T(8,128)(2,1)S(1)}, bf16[1,4,32,1280]{3,2,1,0:T(8,128)(2,1)}, u32[]{:S(2)}) copy-start(bf16[1,4,32,1280]{3,2,1,0:T(8,128)(2,1)} %param.15) | copy-start | bytes 983044
  328.1 132.0 %copy-start.5 = (f32[1280]{0:T(1024)S(1)}, f32[1280]{0:T(1024)}, u32[]{:S(2)}) copy-start(f32[1280]{0:T(1024)} %param.21) | copy-start | bytes 15364
  540.8 2.6 copy-start.1
Sparse Core Ops, SparseCore 0:
  12.0 72.1 all-gather.4
  86.3 239.2 all-gather.6
  328.1 26.6 reduce-scatter.5
  357.2 28.3 reduce-scatter.7
  389.0 71.0 reduce-scatter.3
  461.5 50.1 all-gather.8
